TPU v7x, 32 devices: a whole 2x2x4 slice. The times are simulated.
32 devices in a mesh: row: 4 (over x, core), col: 8 (over z, y).
Axes of the slice: x: 2, y: 2, z: 4, core: 2. Of those that a mesh axis runs over, the one named last changes fastest.
Arguments:
- tiles: bfloat16 [4, 8, 128, 128, 128], P('row', 'col')
- tile_row: int32 [4, 8, 128], P('row', 'col'), may hold values from 0 to 15, as said below
- tile_col: int32 [4, 8, 128], P('row', 'col'), may hold values from 0 to 15
- tile_count: int32 [4, 8], P('row', 'col'), may hold values from 1 to 128, as said below
- sinogram: float32 [4, 2048, 128], P('row', 'col')
Outputs:
- volume: float32 [8, 2048, 128], P('col', 'row')
- residual: float32 [4, 2048, 128], P('row', 'col')
Inputs may be any that keep to these rules, and one draw needn't show every extreme that they name: Within one block the pairs (tile_row, tile_col) of all 128 slots are distinct. Slots 0 to tile_count - 1 of a block are live, the rest are ignored; some block has all 128 slots live in every draw.
All inputs are finite; a program needn't handle non-finite values.
Results may differ from a plain program's by a relative error of at most 0.015.
Values may be sent and summed in bfloat16 or wider, within the bound.
A program may use at most 64 MiB of HBM per device.

v0:
```python
import jax
import jax.numpy as jnp
from jax import lax
from jax.sharding import PartitionSpec as P

RT = 16
VT = 16
ITERS = 4


def frame_squares(values):
    return jnp.sum(values * values, axis=(0, 1))


def forward_local(blocks, rows_index, cols_index, count, voxel_block):
    tile = blocks.shape[1]
    frames = voxel_block.shape[1]
    voxel_tiles = voxel_block.reshape(voxel_block.shape[0] // tile, tile, frames)
    picked = jnp.take(voxel_tiles, cols_index, axis=0)
    products = jnp.einsum("tij,tjk->tik", blocks, picked, preferred_element_type=jnp.float32)
    live = jnp.arange(blocks.shape[0], dtype=jnp.int32) < count
    select = (
        (rows_index[None, :] == jnp.arange(RT, dtype=jnp.int32)[:, None]) & live[None, :]
    ).astype(jnp.float32)
    summed = jnp.einsum("ut,tik->uik", select, products, precision=lax.Precision.HIGHEST)
    return summed.reshape(RT * tile, frames)


def backward_local(blocks, rows_index, cols_index, count, ray_block):
    tile = blocks.shape[1]
    frames = ray_block.shape[1]
    ray_tiles = ray_block.reshape(ray_block.shape[0] // tile, tile, frames)
    picked = jnp.take(ray_tiles, rows_index, axis=0)
    products = jnp.einsum("tji,tjk->tik", blocks, picked, preferred_element_type=jnp.float32)
    live = jnp.arange(blocks.shape[0], dtype=jnp.int32) < count
    select = (
        (cols_index[None, :] == jnp.arange(VT, dtype=jnp.int32)[:, None]) & live[None, :]
    ).astype(jnp.float32)
    summed = jnp.einsum("ut,tik->uik", select, products, precision=lax.Precision.HIGHEST)
    return summed.reshape(VT * tile, frames)


def local(tiles, tile_row, tile_col, tile_count, sinogram):
    blocks = tiles[0, 0]
    rows_index = tile_row[0, 0]
    cols_index = tile_col[0, 0]
    count = tile_count[0, 0]
    tile = blocks.shape[1]
    frames = sinogram.shape[2]
    voxel_piece = VT * tile // lax.axis_size("row")
    ray_piece = RT * tile // lax.axis_size("col")

    def ray_block_of(state):
        return state[0].astype(jnp.bfloat16)

    def voxel_total(term):
        return lax.psum(term, "row")

    residual = lax.all_gather(sinogram, "col", axis=1, tiled=True)
    volume = jnp.zeros((1, VT * tile, frames), jnp.float32)

    def backward(state):
        return voxel_total(
            backward_local(blocks, rows_index, cols_index, count, ray_block_of(state))[None]
        )

    search = backward(residual)
    gamma = lax.psum(frame_squares(search), "col")
    direction = search
    for step in range(ITERS):
        image = lax.psum(
            forward_local(blocks, rows_index, cols_index, count, direction[0].astype(jnp.bfloat16))[
                None
            ],
            "col",
        )
        alpha = gamma / lax.psum(frame_squares(image), "row")
        volume = volume + alpha * direction
        residual = residual - alpha * image
        if step + 1 < ITERS:
            search = backward(residual)
            fresh = lax.psum(frame_squares(search), "col")
            direction = search + fresh / gamma * direction
            gamma = fresh
    return (
        lax.dynamic_slice_in_dim(volume, lax.axis_index("row") * voxel_piece, voxel_piece, 1),
        lax.dynamic_slice_in_dim(residual, lax.axis_index("col") * ray_piece, ray_piece, 1),
    )


def solution(mesh):
    return jax.shard_map(
        local,
        mesh=mesh,
        in_specs=(
            P("row", "col", None, None, None),
            P("row", "col", None),
            P("row", "col", None),
            P("row", "col"),
            P("row", "col", None),
        ),
        out_specs=(P("col", "row", None), P("row", "col", None)),
        check_vma=False,
    )
```

profile of v0, /device:TPU:0, one launch (start us, length us, event | category | flops | bytes accessed | tf_op | source)
XLA Modules:
  0.0 851.0 jit_solution(9143394102961914901)
XLA Ops:
  9.9 43.2 %all-gather.2.cloned.1.call-done = f32[1,2048,128]{2,1,0:T(8,128)} async-done(((f32[1,256,128]{2,1,0:T(8,128)}), f32[1,2048,128]{2,1,0:T(8,128)}) %all-gather.2.cloned.1.call-update) | async-done | bytes 1048592 | tf_op jit(solution)/shard_map/all_gather | solution.py:59
  54.4 3.1 gather_fusion
  57.5 8.4 fusion.30
  65.8 9.3 %copy.15 = f32[128,128,128]{1,0,2:T(8,128)} copy(f32[128,128,128]{2,1,0:T(8,128)} %fusion.30) | data formatting | bytes 16777216 | tf_op jit(solution)/shard_map/tji,tjk->tik/dot_general | solution.py:34
  75.1 5.2 fusion.14
  81.7 35.1 %all-reduce.9.cloned.1.call-done = f32[1,2048,128]{2,1,0:T(8,128)} async-done(((f32[1,2048,128]{2,1,0:T(8,128)}), f32[1,2048,128]{2,1,0:T(8,128)}) %all-reduce.9.cloned.1.call-update) | async-done | bytes 1048592 | tf_op jit(solution)/shard_map/psum | solution.py:57
  118.7 3.1 gather_fusion.1
  121.8 9.9 %fusion.28 = f32[128,128,128]{2,1,0:T(8,128)} fusion(bf16[1,1,128,128,128]{4,3,2,1,0:T(8,128)(2,1)} %param.7, bf16[128,128,128]{2,1,0:T(8,128)(2,1)} %gather_fusion.1, pred[128]{0:T(512)(128)(4,1)S(1)} %get-tuple-element.15), kind=kOutput, calls=%fused_computation.36 | convolution fusion | flops 538968064 | bytes 16777344 | tf_op jit(solution)/shard_map/tij,tjk->tik/dot_general | solution.py:20
  131.7 9.3 %copy.16 = f32[128,128,128]{1,0,2:T(8,128)} copy(f32[128,128,128]{2,1,0:T(8,128)} %fusion.28) | data formatting | bytes 16777216 | tf_op jit(solution)/shard_map/tij,tjk->tik/dot_general | solution.py:20
  141.0 5.2 fusion.12
  147.5 21.7 %psum.113 = f32[128]{0:T(128)S(1)} all-reduce(f32[128]{0:T(128)S(1)} %get-tuple-element.13), channel_id=1, replica_groups=mesh['row'=4,'col'=8] {'col'}, use_global_device_ids=true, to_apply=%region_2.4 | all-reduce | flops 128 | bytes 1024 | tf_op jit(solution)/shard_map/psum | solution.py:68
  169.2 57.2 %all-reduce.11.cloned.1.call-done = f32[1,2048,128]{2,1,0:T(8,128)} async-done(((f32[1,2048,128]{2,1,0:T(8,128)}), f32[1,2048,128]{2,1,0:T(8,128)}) %all-reduce.11.cloned.1.call-update) | async-done | bytes 1048592 | tf_op jit(solution)/shard_map/psum | solution.py:71
  227.9 7.0 psum.115
  236.3 3.1 gather_fusion.2
  239.3 8.4 fusion.26
  247.7 9.3 %copy.17 = f32[128,128,128]{1,0,2:T(8,128)} copy(f32[128,128,128]{2,1,0:T(8,128)} %fusion.26) | data formatting | bytes 16777216 | tf_op jit(solution)/shard_map/tji,tjk->tik/dot_general | solution.py:34
  256.9 5.2 fusion.10
  263.5 35.4 %all-reduce.13.cloned.1.call-done = f32[1,2048,128]{2,1,0:T(8,128)} async-done(((f32[1,2048,128]{2,1,0:T(8,128)}), f32[1,2048,128]{2,1,0:T(8,128)}) %all-reduce.13.cloned.1.call-update) | async-done | bytes 1048592 | tf_op jit(solution)/shard_map/psum | solution.py:57
  300.5 21.4 %psum.117 = f32[128]{0:T(128)S(1)} all-reduce(f32[128]{0:T(128)S(1)} %multiply_reduce_fusion.5), channel_id=1, replica_groups=mesh['row'=4,'col'=8] {'col'}, use_global_device_ids=true, to_apply=%region_8.10 | all-reduce | flops 128 | bytes 1024 | tf_op jit(solution)/shard_map/psum | solution.py:82
  327.3 9.9 %fusion.24 = f32[128,128,128]{2,1,0:T(8,128)} fusion(bf16[1,1,128,128,128]{4,3,2,1,0:T(8,128)(2,1)} %param.7, bf16[128,128,128]{2,1,0:T(8,128)(2,1)} %gather_fusion.3, pred[128]{0:T(512)(128)(4,1)S(1)} %get-tuple-element.15), kind=kOutput, calls=%fused_computation.32 | convolution fusion | flops 538968064 | bytes 16777344 | tf_op jit(solution)/shard_map/tij,tjk->tik/dot_general | solution.py:20
  337.2 9.3 %copy.18 = f32[128,128,128]{1,0,2:T(8,128)} copy(f32[128,128,128]{2,1,0:T(8,128)} %fusion.24) | data formatting | bytes 16777216 | tf_op jit(solution)/shard_map/tij,tjk->tik/dot_general | solution.py:20
  346.4 5.2 fusion.8
  353.0 75.2 %all-reduce.15.cloned.1.call-done = f32[1,2048,128]{2,1,0:T(8,128)} async-done(((f32[1,2048,128]{2,1,0:T(8,128)}), f32[1,2048,128]{2,1,0:T(8,128)}) %all-reduce.15.cloned.1.call-update) | async-done | bytes 1048592 | tf_op jit(solution)/shard_map/psum | solution.py:71
  429.8 6.7 psum.119
  438.9 3.1 gather_fusion.4
  442.0 8.4 fusion.22
  450.3 9.3 %copy.19 = f32[128,128,128]{1,0,2:T(8,128)} copy(f32[128,128,128]{2,1,0:T(8,128)} %fusion.22) | data formatting | bytes 16777216 | tf_op jit(solution)/shard_map/tji,tjk->tik/dot_general | solution.py:34
  459.6 5.2 fusion.6
  466.2 35.4 %all-reduce.17.cloned.1.call-done = f32[1,2048,128]{2,1,0:T(8,128)} async-done(((f32[1,2048,128]{2,1,0:T(8,128)}), f32[1,2048,128]{2,1,0:T(8,128)}) %all-reduce.17.cloned.1.call-update) | async-done | bytes 1048592 | tf_op jit(solution)/shard_map/psum | solution.py:57
  503.1 21.4 %psum.121 = f32[128]{0:T(128)S(1)} all-reduce(f32[128]{0:T(128)S(1)} %multiply_reduce_fusion.3), channel_id=1, replica_groups=mesh['row'=4,'col'=8] {'col'}, use_global_device_ids=true, to_apply=%region_14.16 | all-reduce | flops 128 | bytes 1024 | tf_op jit(solution)/shard_map/psum | solution.py:82
  525.9 3.1 gather_fusion.5
  528.9 9.9 %fusion.20 = f32[128,128,128]{2,1,0:T(8,128)} fusion(bf16[1,1,128,128,128]{4,3,2,1,0:T(8,128)(2,1)} %param.7, bf16[128,128,128]{2,1,0:T(8,128)(2,1)} %gather_fusion.5, pred[128]{0:T(512)(128)(4,1)S(1)} %get-tuple-element.15), kind=kOutput, calls=%fused_computation.28 | convolution fusion | flops 538968064 | bytes 16777344 | tf_op jit(solution)/shard_map/tij,tjk->tik/dot_general | solution.py:20
  538.8 9.3 %copy.20 = f32[128,128,128]{1,0,2:T(8,128)} copy(f32[128,128,128]{2,1,0:T(8,128)} %fusion.20) | data formatting | bytes 16777216 | tf_op jit(solution)/shard_map/tij,tjk->tik/dot_general | solution.py:20
  548.1 5.2 fusion.4
  554.7 75.1 %all-reduce.19.cloned.1.call-done = f32[1,2048,128]{2,1,0:T(8,128)} async-done(((f32[1,2048,128]{2,1,0:T(8,128)}), f32[1,2048,128]{2,1,0:T(8,128)}) %all-reduce.19.cloned.1.call-update) | async-done | bytes 1048592 | tf_op jit(solution)/shard_map/psum | solution.py:71
  631.3 6.7 psum.123
  640.7 3.1 gather_fusion.6
  643.8 8.4 fusion.18
  652.2 9.3 %copy.21 = f32[128,128,128]{1,0,2:T(8,128)} copy(f32[128,128,128]{2,1,0:T(8,128)} %fusion.18) | data formatting | bytes 16777216 | tf_op jit(solution)/shard_map/tji,tjk->tik/dot_general | solution.py:34
  661.4 5.2 fusion.2
  668.0 35.4 %all-reduce.21.cloned.1.call-done = f32[1,2048,128]{2,1,0:T(8,128)} async-done(((f32[1,2048,128]{2,1,0:T(8,128)}), f32[1,2048,128]{2,1,0:T(8,128)}) %all-reduce.21.cloned.1.call-update) | async-done | bytes 1048592 | tf_op jit(solution)/shard_map/psum | solution.py:57
  704.9 21.4 %psum.125 = f32[128]{0:T(128)S(1)} all-reduce(f32[128]{0:T(128)S(1)} %multiply_reduce_fusion.1), channel_id=1, replica_groups=mesh['row'=4,'col'=8] {'col'}, use_global_device_ids=true, to_apply=%region_20.22 | all-reduce | flops 128 | bytes 1024 | tf_op jit(solution)/shard_map/psum | solution.py:82
  728.7 3.1 gather_fusion.7
  731.8 9.9 %fusion.16 = f32[128,128,128]{2,1,0:T(8,128)} fusion(bf16[1,1,128,128,128]{4,3,2,1,0:T(8,128)(2,1)} %param.7, bf16[128,128,128]{2,1,0:T(8,128)(2,1)} %gather_fusion.7, pred[128]{0:T(512)(128)(4,1)S(1)} %get-tuple-element.15), kind=kOutput, calls=%fused_computation.24 | convolution fusion | flops 538968064 | bytes 16777344 | tf_op jit(solution)/shard_map/tij,tjk->tik/dot_general | solution.py:20
  741.7 9.3 %copy.22 = f32[128,128,128]{1,0,2:T(8,128)} copy(f32[128,128,128]{2,1,0:T(8,128)} %fusion.16) | data formatting | bytes 16777216 | tf_op jit(solution)/shard_map/tij,tjk->tik/dot_general | solution.py:20
  750.9 5.2 fusion
  757.5 75.3 %all-reduce.23.cloned.1.call-done = f32[1,2048,128]{2,1,0:T(8,128)} async-done(((f32[1,2048,128]{2,1,0:T(8,128)}), f32[1,2048,128]{2,1,0:T(8,128)}) %all-reduce.23.cloned.1.call-update) | async-done | bytes 1048592 | tf_op jit(solution)/shard_map/psum | solution.py:71
  834.3 6.5 psum.127
  (69 shorter events, 46.2 us)
Async XLA Ops:
  7.2 46.0 %all-gather.2.cloned.1.call-start = ((), (), s32[]{:S(2)}) async-start(), calls=%async_computation | async-start | bytes 1179648 | tf_op jit(solution)/shard_map/all_gather | solution.py:59
  7.9 108.9 %all-reduce.9.cloned.1.call-start = ((), (), s32[]{:S(2)}) async-start(), calls=%async_computation.1 | async-start | bytes 2097152 | tf_op jit(solution)/shard_map/psum | solution.py:57
  65.8 9.3 %copy-start.4 = (s32[1,1,128]{2,1,0:T(1,128)S(1)}, s32[1,1,128]{2,1,0:T(1,128)}, u32[]{:S(2)}) copy-start(s32[1,1,128]{2,1,0:T(1,128)} %param.9) | copy-start | bytes 1540
  81.7 144.8 %all-reduce.11.cloned.1.call-start = ((), (), s32[]{:S(2)}) async-start(), calls=%async_computation.2 | async-start | bytes 2097152 | tf_op jit(solution)/shard_map/psum | solution.py:71
  131.7 9.3 %copy-start.5 = (s32[1,1,128]{2,1,0:T(1,128)S(1)}, s32[1,1,128]{2,1,0:T(1,128)}, u32[]{:S(2)}) copy-start(s32[1,1,128]{2,1,0:T(1,128)} %param.8) | copy-start | bytes 1540
  146.1 88.8 %copy-start = (f32[1,2048,128]{2,1,0:T(8,128)S(1)}, f32[1,2048,128]{2,1,0:T(8,128)}, u32[]{:S(2)}) copy-start(f32[1,2048,128]{2,1,0:T(8,128)} %all-gather.2.cloned.1.call-done) | copy-start | bytes 3145732
  147.5 151.5 %all-reduce.13.cloned.1.call-start = ((), (), s32[]{:S(2)}) async-start(), calls=%async_computation.3 | async-start | bytes 2097152 | tf_op jit(solution)/shard_map/psum | solution.py:57
  262.1 59.7 %copy-start.2 = (f32[1,2048,128]{2,1,0:T(8,128)S(1)}, f32[1,2048,128]{2,1,0:T(8,128)}, u32[]{:S(2)}) copy-start(f32[1,2048,128]{2,1,0:T(8,128)} %all-reduce.9.cloned.1.call-done) | copy-start | bytes 3145732
  263.5 164.8 %all-reduce.15.cloned.1.call-start = ((), (), s32[]{:S(2)}) async-start(), calls=%async_computation.4 | async-start | bytes 2097152 | tf_op jit(solution)/shard_map/psum | solution.py:71
  351.6 84.9 %copy-start.1 = (f32[1,2048,128]{2,1,0:T(8,128)S(1)}, f32[1,2048,128]{2,1,0:T(8,128)}, u32[]{:S(2)}) copy-start(f32[1,2048,128]{2,1,0:T(8,128)} %all-reduce.11.cloned.1.call-done) | copy-start | bytes 3145732
  353.0 148.6 %all-reduce.17.cloned.1.call-start = ((), (), s32[]{:S(2)}) async-start(), calls=%async_computation.5 | async-start | bytes 2097152 | tf_op jit(solution)/shard_map/psum | solution.py:57
  464.8 59.7 %copy-start.3 = (f32[1,2048,128]{2,1,0:T(8,128)S(1)}, f32[1,2048,128]{2,1,0:T(8,128)}, u32[]{:S(2)}) copy-start(f32[1,2048,128]{2,1,0:T(8,128)} %get-tuple-element.12) | copy-start | bytes 3145732
  466.1 163.7 %all-reduce.19.cloned.1.call-start = ((), (), s32[]{:S(2)}) async-start(), calls=%async_computation.6 | async-start | bytes 2097152 | tf_op jit(solution)/shard_map/psum | solution.py:71
  554.6 148.8 %all-reduce.21.cloned.1.call-start = ((), (), s32[]{:S(2)}) async-start(), calls=%async_computation.7 | async-start | bytes 2097152 | tf_op jit(solution)/shard_map/psum | solution.py:57
  668.0 164.8 %all-reduce.23.cloned.1.call-start = ((), (), s32[]{:S(2)}) async-start(), calls=%async_computation.8 | async-start | bytes 2097152 | tf_op jit(solution)/shard_map/psum | solution.py:71
Sparse Core Ops, SparseCore 0:
  10.1 42.9 all-gather.1
  81.8 34.9 all-reduce.8
  147.6 78.7 all-reduce.10
  263.6 35.3 all-reduce.12
  353.1 75.1 all-reduce.14
  466.3 35.3 all-reduce.16
  554.8 75.0 all-reduce.18
  668.1 35.3 all-reduce.20
  757.6 75.1 all-reduce.22
where the time goes:
time: 861 us; the launch traced here: 851 us
  waiting for transfers between devices  468 us (54%)
  matrix products  114 us (13%)
  blocking collectives  113 us (13%)
  local copies, waits for them, and re-layouts  109 us (13%)
  other arithmetic  31.2 us (4%)
  between operations  14.9 us (2%)
    psum x4, waiting for transfers between devices, local(): lax.psum(forward_local(blocks, rows_index, cols_index, count, direction[0...  283 us
    psum x4, waiting for transfers between devices, voxel_total(): return lax.psum(term, 'row')  141 us
    psum x3, blocking collectives, local(): fresh = lax.psum(frame_squares(search), 'col')  64.1 us
    all_gather x1, waiting for transfers between devices, local(): residual = lax.all_gather(sinogram, 'col', axis=1, tiled=True)  43.2 us
    dot_general x4, matrix products, forward_local(): jnp.einsum('tij,tjk->tik', blocks, picked, preferred_element_type=jnp.flo...  39.7 us
    dot_general x4, local copies, waits for them, and re-layouts, backward_local(): jnp.einsum('tji,tjk->tik', blocks, picked, preferred_element_type=jnp.flo...  37.1 us
    dot_general x4, local copies, waits for them, and re-layouts, forward_local(): jnp.einsum('tij,tjk->tik', blocks, picked, preferred_element_type=jnp.flo...  37.1 us
    dot_general x4, matrix products, backward_local(): jnp.einsum('tji,tjk->tik', blocks, picked, preferred_element_type=jnp.flo...  33.5 us
  transfers between devices with their start and end apart: 9, of which 9 were waited for; matrix products, arithmetic and copies ran while one was open for 0% of the time, Pallas kernels for 0%

commit v1 on v0

--- a/solution.py
+++ b/solution.py
@@ -68,11 +68,11 @@
     gamma = lax.psum(frame_squares(search), "col")
     direction = search
     for step in range(ITERS):
-        image = lax.psum(
+        save_ladders_on = lambda a0: jnp.sum(lax.all_gather(a0, "col"), axis=0)
+        image = save_ladders_on(
             forward_local(blocks, rows_index, cols_index, count, direction[0].astype(jnp.bfloat16))[
                 None
-            ],
-            "col",
+            ]
         )
         alpha = gamma / lax.psum(frame_squares(image), "row")
         volume = volume + alpha * direction

time: 861 us -> 1050 us (1.22)
  waiting for transfers between devices: 468 us -> 650 us
  other arithmetic: 31.2 us -> 43.6 us
    all_gather x0 -> x4, waiting for transfers between devices: none -> 467 us  [local(): save_ladders_on = lambda a0: jnp.sum(lax.all_gather(a0, 'col'), axis=0)]
    psum x4 -> x0, waiting for transfers between devices: 283 us -> none  [local(): lax.psum(forward_local(blocks, rows_index, cols_index, count, direction[0...]
    reduce_sum x0 -> x4, other arithmetic: none -> 16.7 us  [local(): save_ladders_on = lambda a0: jnp.sum(lax.all_gather(a0, 'col'), axis=0)]
where the time goes in v1:
time: 1050 us; the launch traced here: 1040 us
  waiting for transfers between devices  650 us (62%)
  matrix products  114 us (11%)
  blocking collectives  110 us (10%)
  local copies, waits for them, and re-layouts  109 us (10%)
  other arithmetic  43.6 us (4%)
  between operations  14.9 us (1%)
    all_gather x4, waiting for transfers between devices, local(): save_ladders_on = lambda a0: jnp.sum(lax.all_gather(a0, 'col'), axis=0)  467 us
    psum x4, waiting for transfers between devices, voxel_total(): return lax.psum(term, 'row')  139 us
    psum x3, blocking collectives, local(): fresh = lax.psum(frame_squares(search), 'col')  64.1 us
    all_gather x1, waiting for transfers between devices, local(): residual = lax.all_gather(sinogram, 'col', axis=1, tiled=True)  43.2 us
    dot_general x4, matrix products, forward_local(): jnp.einsum('tij,tjk->tik', blocks, picked, preferred_element_type=jnp.flo...  39.7 us
    dot_general x4, local copies, waits for them, and re-layouts, forward_local(): jnp.einsum('tij,tjk->tik', blocks, picked, preferred_element_type=jnp.flo...  37.1 us
    dot_general x4, local copies, waits for them, and re-layouts, backward_local(): jnp.einsum('tji,tjk->tik', blocks, picked, preferred_element_type=jnp.flo...  37.1 us
    dot_general x4, matrix products, backward_local(): jnp.einsum('tji,tjk->tik', blocks, picked, preferred_element_type=jnp.flo...  33.5 us
  transfers between devices with their start and end apart: 9, of which 9 were waited for; matrix products, arithmetic and copies ran while one was open for 0% of the time, Pallas kernels for 0%

profile of v1, /device:TPU:0, one launch (start us, length us, event | category | flops | bytes accessed | tf_op | source)
XLA Modules:
  0.0 1043.1 jit_solution(1926015520991223598)
XLA Ops:
  9.9 43.2 %all-gather.6.cloned.1.call-done = f32[1,2048,128]{2,1,0:T(8,128)} async-done(((f32[1,256,128]{2,1,0:T(8,128)}), f32[1,2048,128]{2,1,0:T(8,128)}) %all-gather.6.cloned.1.call-update) | async-done | bytes 1048592 | tf_op jit(solution)/shard_map/all_gather | solution.py:59
  54.4 3.1 gather_fusion
  57.5 8.4 fusion.32
  65.8 9.3 copy.32
  75.1 5.2 fusion.113
  81.7 35.1 %all-reduce.5.cloned.1.call-done = f32[1,2048,128]{2,1,0:T(8,128)} async-done(((f32[1,2048,128]{2,1,0:T(8,128)}), f32[1,2048,128]{2,1,0:T(8,128)}) %all-reduce.5.cloned.1.call-update) | async-done | bytes 1048592 | tf_op jit(solution)/shard_map/psum | solution.py:57
  118.7 3.1 gather_fusion.1
  121.7 9.9 fusion.37
  131.6 9.3 copy.35
  140.9 5.2 fusion.105
  147.5 22.0 %psum.85 = f32[128]{0:T(128)S(1)} all-reduce(f32[128]{0:T(128)S(1)} %get-tuple-element.13), channel_id=1, replica_groups=mesh['row'=4,'col'=8] {'col'}, use_global_device_ids=true, to_apply=%region_2.4 | all-reduce | flops 128 | bytes 1024 | tf_op jit(solution)/shard_map/psum | solution.py:68
  169.6 103.2 %all-gather.8.cloned.1.call-done = f32[8,1,2048,128]{3,2,1,0:T(8,128)} async-done(((f32[1,1,2048,128]{3,2,1,0:T(8,128)}), f32[8,1,2048,128]{3,2,1,0:T(8,128)}) %all-gather.8.cloned.1.call-update) | async-done | bytes 8388624 | tf_op jit(solution)/shard_map/all_gather | solution.py:71
  272.7 3.9 reduce_sum.117
  276.9 6.3 psum.86
  283.4 3.1 gather_fusion.2
  286.4 8.4 fusion.42
  294.8 9.3 copy.38
  304.1 5.2 fusion.111
  310.6 34.6 %all-reduce.7.cloned.1.call-done = f32[1,2048,128]{2,1,0:T(8,128)} async-done(((f32[1,2048,128]{2,1,0:T(8,128)}), f32[1,2048,128]{2,1,0:T(8,128)}) %all-reduce.7.cloned.1.call-update) | async-done | bytes 1048592 | tf_op jit(solution)/shard_map/psum | solution.py:57
  346.7 21.4 %psum.88 = f32[128]{0:T(128)S(1)} all-reduce(f32[128]{0:T(128)S(1)} %multiply_reduce_fusion.5), channel_id=1, replica_groups=mesh['row'=4,'col'=8] {'col'}, use_global_device_ids=true, to_apply=%region_8.10 | all-reduce | flops 128 | bytes 1024 | tf_op jit(solution)/shard_map/psum | solution.py:82
  373.5 9.9 fusion.47
  383.4 9.3 copy.41
  392.7 5.2 fusion.103
  399.2 121.4 %all-gather.10.cloned.1.call-done = f32[8,1,2048,128]{3,2,1,0:T(8,128)} async-done(((f32[1,1,2048,128]{3,2,1,0:T(8,128)}), f32[8,1,2048,128]{3,2,1,0:T(8,128)}) %all-gather.10.cloned.1.call-update) | async-done | bytes 8388624 | tf_op jit(solution)/shard_map/all_gather | solution.py:71
  520.6 3.9 reduce_sum.121
  524.8 6.0 psum.89
  536.3 8.4 fusion.52
  544.7 9.3 copy.44
  553.9 5.2 fusion.109
  560.5 34.6 %all-reduce.9.cloned.1.call-done = f32[1,2048,128]{2,1,0:T(8,128)} async-done(((f32[1,2048,128]{2,1,0:T(8,128)}), f32[1,2048,128]{2,1,0:T(8,128)}) %all-reduce.9.cloned.1.call-update) | async-done | bytes 1048592 | tf_op jit(solution)/shard_map/psum | solution.py:57
  596.6 21.4 %psum.91 = f32[128]{0:T(128)S(1)} all-reduce(f32[128]{0:T(128)S(1)} %multiply_reduce_fusion.3), channel_id=1, replica_groups=mesh['row'=4,'col'=8] {'col'}, use_global_device_ids=true, to_apply=%region_14.16 | all-reduce | flops 128 | bytes 1024 | tf_op jit(solution)/shard_map/psum | solution.py:82
  623.4 9.9 fusion.57
  633.3 9.3 copy.47
  642.6 5.2 fusion.101
  649.2 121.4 %all-gather.12.cloned.1.call-done = f32[8,1,2048,128]{3,2,1,0:T(8,128)} async-done(((f32[1,1,2048,128]{3,2,1,0:T(8,128)}), f32[8,1,2048,128]{3,2,1,0:T(8,128)}) %all-gather.12.cloned.1.call-update) | async-done | bytes 8388624 | tf_op jit(solution)/shard_map/all_gather | solution.py:71
  770.5 3.9 reduce_sum.125
  774.7 6.1 psum.92
  786.3 8.4 fusion.62
  794.6 9.3 copy.50
  803.9 5.2 fusion.107
  810.4 34.6 %all-reduce.11.cloned.1.call-done = f32[1,2048,128]{2,1,0:T(8,128)} async-done(((f32[1,2048,128]{2,1,0:T(8,128)}), f32[1,2048,128]{2,1,0:T(8,128)}) %all-reduce.11.cloned.1.call-update) | async-done | bytes 1048592 | tf_op jit(solution)/shard_map/psum | solution.py:57
  846.6 21.4 %psum.94 = f32[128]{0:T(128)S(1)} all-reduce(f32[128]{0:T(128)S(1)} %multiply_reduce_fusion.1), channel_id=1, replica_groups=mesh['row'=4,'col'=8] {'col'}, use_global_device_ids=true, to_apply=%region_20.22 | all-reduce | flops 128 | bytes 1024 | tf_op jit(solution)/shard_map/psum | solution.py:82
  873.3 9.9 fusion.67
  883.3 9.3 copy.53
  892.5 5.2 fusion.99
  899.1 121.4 %all-gather.14.cloned.1.call-done = f32[8,1,2048,128]{3,2,1,0:T(8,128)} async-done(((f32[1,1,2048,128]{3,2,1,0:T(8,128)}), f32[8,1,2048,128]{3,2,1,0:T(8,128)}) %all-gather.14.cloned.1.call-update) | async-done | bytes 8388624 | tf_op jit(solution)/shard_map/all_gather | solution.py:71
  1020.5 5.0 reduce_sum.129
  1027.0 5.8 psum.95
  (73 shorter events, 54.1 us)
Async XLA Ops:
  7.2 46.0 %all-gather.6.cloned.1.call-start = ((), (), s32[]{:S(2)}) async-start(), calls=%async_computation | async-start | bytes 1179648 | tf_op jit(solution)/shard_map/all_gather | solution.py:59
  7.9 108.9 %all-reduce.5.cloned.1.call-start = ((), (), s32[]{:S(2)}) async-start(), calls=%async_computation.1 | async-start | bytes 2097152 | tf_op jit(solution)/shard_map/psum | solution.py:57
  65.8 9.3 copy-start.4
  81.6 191.1 %all-gather.8.cloned.1.call-start = ((), (), s32[]{:S(2)}) async-start(), calls=%async_computation.2 | async-start | bytes 9437184 | tf_op jit(solution)/shard_map/all_gather | solution.py:71
  131.6 9.3 copy-start.5
  147.5 197.7 %all-reduce.7.cloned.1.call-start = ((), (), s32[]{:S(2)}) async-start(), calls=%async_computation.3 | async-start | bytes 2097152 | tf_op jit(solution)/shard_map/psum | solution.py:57
  169.6 113.7 %copy-start = (f32[1,2048,128]{2,1,0:T(8,128)S(1)}, f32[1,2048,128]{2,1,0:T(8,128)}, u32[]{:S(2)}) copy-start(f32[1,2048,128]{2,1,0:T(8,128)} %all-gather.6.cloned.1.call-done) | copy-start | bytes 3145732
  309.2 58.9 %copy-start.1 = (f32[1,2048,128]{2,1,0:T(8,128)S(1)}, f32[1,2048,128]{2,1,0:T(8,128)}, u32[]{:S(2)}) copy-start(f32[1,2048,128]{2,1,0:T(8,128)} %all-reduce.5.cloned.1.call-done) | copy-start | bytes 3145732
  310.6 210.1 %all-gather.10.cloned.1.call-start = ((), (), s32[]{:S(2)}) async-start(), calls=%async_computation.4 | async-start | bytes 9437184 | tf_op jit(solution)/shard_map/all_gather | solution.py:71
  399.2 195.9 %all-reduce.9.cloned.1.call-start = ((), (), s32[]{:S(2)}) async-start(), calls=%async_computation.5 | async-start | bytes 2097152 | tf_op jit(solution)/shard_map/psum | solution.py:57
  559.1 58.9 %copy-start.2 = (f32[1,2048,128]{2,1,0:T(8,128)S(1)}, f32[1,2048,128]{2,1,0:T(8,128)}, u32[]{:S(2)}) copy-start(f32[1,2048,128]{2,1,0:T(8,128)} %get-tuple-element.12) | copy-start | bytes 3145732
  560.4 210.1 %all-gather.12.cloned.1.call-start = ((), (), s32[]{:S(2)}) async-start(), calls=%async_computation.6 | async-start | bytes 9437184 | tf_op jit(solution)/shard_map/all_gather | solution.py:71
  649.1 196.0 %all-reduce.11.cloned.1.call-start = ((), (), s32[]{:S(2)}) async-start(), calls=%async_computation.7 | async-start | bytes 2097152 | tf_op jit(solution)/shard_map/psum | solution.py:57
  809.0 58.9 %copy-start.3 = (f32[1,2048,128]{2,1,0:T(8,128)S(1)}, f32[1,2048,128]{2,1,0:T(8,128)}, u32[]{:S(2)}) copy-start(f32[1,2048,128]{2,1,0:T(8,128)} %get-tuple-element.8) | copy-start | bytes 3145732
  810.4 210.1 %all-gather.14.cloned.1.call-start = ((), (), s32[]{:S(2)}) async-start(), calls=%async_computation.8 | async-start | bytes 9437184 | tf_op jit(solution)/shard_map/all_gather | solution.py:71
Sparse Core Ops, SparseCore 0:
  10.1 42.9 all-gather.5
  81.7 34.9 all-reduce.4
  147.6 125.0 all-gather.7
  310.7 34.5 all-reduce.6
  399.3 121.2 all-gather.9
  560.6 34.5 all-reduce.8
  649.2 121.2 all-gather.11
  810.5 34.5 all-reduce.10
  899.2 121.2 all-gather.13
